TPU v7x, 32 devices: a whole 2x2x4 slice. The times are simulated.
32 devices in a mesh: gx: 4 (over z), gy: 4 (over x, core), gz: 2 (over y).
Axes of the slice: x: 2, y: 2, z: 4, core: 2. Of those that a mesh axis runs over, the one named last changes fastest.
Arguments:
- x_a: bfloat16 [32, 8, 64, 256], P(None, 'gx', 'gy', 'gz'), may hold values from -12 to 12
- x_b: bfloat16 [32, 8, 64, 256], P(None, 'gx', 'gy', 'gz'), may hold values from -12 to 12
- w_first: bfloat16 [3, 3, 3, 32, 32], replicated, may hold values from -0.21875 to 0.21875
- w_second: bfloat16 [3, 3, 3, 32, 32], replicated, may hold values from -0.21875 to 0.21875
- gain_first: float32 [32], replicated, may hold values from 0.1 to 1.9
- bias_first: float32 [32], replicated, may hold values from -2 to 2
- gain_second: float32 [32], replicated, may hold values from 0.1 to 1.9
- bias_second: float32 [32], replicated, may hold values from -2 to 2
- grad_out: bfloat16 [32, 8, 64, 256], P(None, 'gx', 'gy', 'gz'), may hold values from -6 to 6
Outputs:
- y_a: bfloat16 [32, 8, 64, 256], P(None, 'gx', 'gy', 'gz')
- dx_b: bfloat16 [32, 8, 64, 256], P(None, 'gx', 'gy', 'gz')
- grad_w_first: float32 [3, 3, 3, 32, 32], replicated
- grad_w_second: float32 [3, 3, 3, 32, 32], replicated
- grad_norm: float32 [4, 32], replicated
All inputs are finite; a program needn't handle non-finite values.
Results may differ from a plain program's by a relative error of at most 0.0063.
Values may be sent and summed in bfloat16 or wider, within the bound.
No kernel may reach another device: no remote copies, remote signals or barrier semaphores. Data moves between devices by JAX's collectives and lax.ppermute only.
A program may use at most 128 MiB of HBM per device.

v0:
```python
import math
import jax
import jax.numpy as jnp
from jax import lax
from jax.sharding import PartitionSpec as P

EPSILON = 1e-05


def extended(block, sides, width):
    for axis, dim in sides:
        count = lax.axis_size(axis)
        forward = [(i, i + 1) for i in range(count - 1)]
        backward = [(target, source) for source, target in forward]
        low = lax.ppermute(
            lax.slice_in_dim(block, block.shape[dim] - width, None, axis=dim), axis, forward
        )
        high = lax.ppermute(lax.slice_in_dim(block, 0, width, axis=dim), axis, backward)
        block = jnp.concatenate([low, block, high], axis=dim)
    return block


def spread(values):
    return values[:, None, None, None]


def silu_slope(value):
    sigma = jax.nn.sigmoid(value)
    return sigma * (1.0 + value * (1.0 - sigma))


def convolve(padded, weight):
    in_chan = padded.shape[0]
    out_chan = weight.shape[3]
    span_x = padded.shape[1] - 2
    span_y = padded.shape[2] - 2
    span_z = padded.shape[3] - 2
    total = jnp.zeros((out_chan, span_x * span_y * span_z), jnp.float32)
    for shift_x in range(3):
        for shift_y in range(3):
            pieces = [
                padded[
                    :,
                    shift_x : shift_x + span_x,
                    shift_y : shift_y + span_y,
                    shift_z : shift_z + span_z,
                ]
                for shift_z in range(3)
            ]
            stacked = jnp.concatenate(pieces, axis=0).reshape(3 * in_chan, -1)
            matrix = weight[shift_x, shift_y].transpose(1, 0, 2).reshape(out_chan, 3 * in_chan)
            total = total + jnp.dot(matrix, stacked, preferred_element_type=jnp.float32)
    return total.reshape(out_chan, span_x, span_y, span_z)


def kernel_grad(padded, upstream):
    in_chan = padded.shape[0]
    out_chan = upstream.shape[0]
    span_x, span_y, span_z = (upstream.shape[1], upstream.shape[2], upstream.shape[3])
    flat = upstream.reshape(out_chan, -1)
    rows = []
    for shift_x in range(3):
        for shift_y in range(3):
            pieces = [
                padded[
                    :,
                    shift_x : shift_x + span_x,
                    shift_y : shift_y + span_y,
                    shift_z : shift_z + span_z,
                ]
                for shift_z in range(3)
            ]
            stacked = jnp.concatenate(pieces, axis=0).reshape(3 * in_chan, -1)
            product = lax.dot_general(
                flat, stacked, (((1,), (1,)), ((), ())), preferred_element_type=jnp.float32
            )
            rows.append(product.reshape(out_chan, 3, in_chan).transpose(1, 0, 2))
    return jnp.stack(rows).reshape(3, 3, 3, out_chan, in_chan)


def flipped(weight):
    return jnp.flip(weight, (0, 1, 2)).transpose(0, 1, 2, 4, 3)


def statistics(blocks, voxels):
    local_sums = jnp.stack([jnp.sum(block, axis=(1, 2, 3)) for block in blocks])
    local_squares = jnp.stack([jnp.sum(jnp.square(block), axis=(1, 2, 3)) for block in blocks])
    sums, squares = lax.psum((local_sums, local_squares), ("gx", "gy", "gz"))
    means = sums / voxels
    variance = squares / voxels - means * means
    return (means, lax.rsqrt(variance + EPSILON))


def normalize(block, means, scales, gain, bias):
    normed = (block - spread(means)) * spread(scales)
    return (normed, spread(gain) * normed + spread(bias))


def backward_layer(upstream, preact, normed, scales, gain, voxels):
    slope = upstream * silu_slope(preact)
    sum_d, sum_dx = lax.psum(
        (jnp.sum(slope, axis=(1, 2, 3)), jnp.sum(slope * normed, axis=(1, 2, 3))),
        ("gx", "gy", "gz"),
    )
    delta = spread(gain * scales) * (
        slope - spread(sum_d / voxels) - normed * spread(sum_dx / voxels)
    )
    return (delta.astype(jnp.bfloat16), sum_d, sum_dx)


def body(x_a, x_b, w_first, w_second, gain_first, bias_first, gain_second, bias_second, grad_out):
    rows_x, rows_y, rows_z = (x_a.shape[1], x_a.shape[2], x_a.shape[3])
    voxels = float(
        rows_x * rows_y * rows_z * lax.axis_size("gx") * lax.axis_size("gy") * lax.axis_size("gz")
    )
    factor = 1.0 / math.sqrt(voxels)
    volumes = jnp.stack([x_a, x_b])
    padded = extended(volumes, (("gx", 2), ("gy", 3), ("gz", 4)), 1)
    first = [convolve(padded[member], w_first) for member in range(2)]
    means, scales = statistics(first, voxels)
    hidden = []
    for member in range(2):
        normed, preact = normalize(
            first[member], means[member], scales[member], gain_first, bias_first
        )
        hidden.append((preact * jax.nn.sigmoid(preact)).astype(jnp.bfloat16))
    hidden_all = extended(jnp.stack(hidden), (("gx", 2), ("gy", 3), ("gz", 4)), 1)
    hidden_pads = [hidden_all[0], hidden_all[1]]
    input_pad_b = padded[1]
    scale_one = scales[1]
    second = [convolve(hidden_pads[member], w_second) for member in range(2)]
    means_two, scales_two = statistics(second, voxels)
    normed_a, preact_a = normalize(second[0], means_two[0], scales_two[0], gain_second, bias_second)
    y_a = (preact_a * jax.nn.sigmoid(preact_a)).astype(jnp.bfloat16)
    norm_two, pre_two = normalize(second[1], means_two[1], scales_two[1], gain_second, bias_second)
    delta_two, sum_d2, sum_x2 = backward_layer(
        grad_out.astype(jnp.float32), pre_two, norm_two, scales_two[1], gain_second, voxels
    )
    local_second = kernel_grad(hidden_pads[1], delta_two) * factor
    grad_w_second = lax.psum(local_second, ("gx", "gy", "gz"))
    delta_pad_two = extended(delta_two, (("gx", 1), ("gy", 2), ("gz", 3)), 1)
    upstream_one = convolve(delta_pad_two, flipped(w_second))
    delta_one, sum_d1, sum_x1 = backward_layer(
        upstream_one, preact, normed, scale_one, gain_first, voxels
    )
    local_first = kernel_grad(input_pad_b, delta_one) * factor
    delta_pad_one = extended(delta_one, (("gx", 1), ("gy", 2), ("gz", 3)), 1)
    dx_b = convolve(delta_pad_one, flipped(w_first)).astype(jnp.bfloat16)
    grad_w_first = lax.psum(local_first, ("gx", "gy", "gz"))
    grad_norm = jnp.stack([sum_x1, sum_d1, sum_x2, sum_d2]) * factor
    return (y_a, dx_b, grad_w_first, grad_w_second, grad_norm)


def solution(mesh):
    placed = (
        P(None, "gx", "gy", "gz"),
        P(None, "gx", "gy", "gz"),
        P(),
        P(),
        P(),
        P(),
        P(),
        P(),
        P(None, "gx", "gy", "gz"),
    )
    return jax.shard_map(
        body,
        mesh=mesh,
        in_specs=placed,
        out_specs=(P(None, "gx", "gy", "gz"), P(None, "gx", "gy", "gz"), P(), P(), P()),
        check_vma=False,
    )
```

profile of v0, /device:TPU:0, one launch (start us, length us, event | category | flops | bytes accessed | tf_op | source)
XLA Modules:
  0.0 585.4 jit_solution(11531565275628670312)
XLA Ops:
  8.4 5.0 collective-permute-start
  15.6 3.3 collective-permute-done
  18.9 4.1 collective-permute-done.1
  23.2 3.7 copy.460
  31.5 3.1 collective-permute-done.3
  34.6 6.2 %pad_maximum_fusion = bf16[2,32,4,18,128]{1,2,4,3,0:T(4,128)(2,1)S(1)} fusion(bf16[2,32,4,1,128]{1,2,4,3,0:T(4,128)(2,1)S(1)} %collective-permute-done.3, bf16[2,32,4,16,128]{1,2,4,3,0:T(4,128)(2,1)} %copy.460, bf16[2,32,4,1,128]{1,2,4,3,0:T(4,128)(2,1)S(1)} %collective-permute-done.2), kind=kLoop, calls=%fused_computation | loop fusion | flops 1179648 | bytes 2359296 | tf_op jit(solution)/shard_map/concatenate | solution.py:19
  43.0 4.0 collective-permute-start.4
  54.2 6.3 %copy.464 = bf16[2,32,4,18,128]{4,1,3,2,0:T(8,128)(2,1)S(1)} copy(bf16[2,32,4,18,128]{1,2,4,3,0:T(4,128)(2,1)} %copy-done) | data formatting | bytes 2359296 | tf_op jit(solution)/shard_map/concatenate | solution.py:19
  67.7 3.2 fusion.175
  94.8 44.5 %all-reduce.3 = (f32[2,32]{1,0:T(2,128)S(1)}, f32[2,32]{1,0:T(2,128)S(1)}) all-reduce(f32[2,32]{1,0:T(2,128)S(1)} %pad_maximum_fusion.75, f32[2,32]{1,0:T(2,128)S(1)} %pad_maximum_fusion.74), channel_id=1, replica_groups=mesh['gx'=4,'gy'=4,'gz'=2] {'gx','gy','gz'}, use_global_device_ids=true, to_apply=%region_5.0 | all-reduce | flops 128 | bytes 1024 | tf_op jit(solution)/shard_map/psum | solution.py:88
  145.9 2.7 collective-permute-done.6
  148.5 4.1 collective-permute-done.7
  153.8 5.6 copy.493
  169.8 6.3 %pad_maximum_fusion.1 = bf16[2,32,4,18,128]{1,2,4,3,0:T(4,128)(2,1)S(1)} fusion(bf16[2,32,4,1,128]{1,2,4,3,0:T(4,128)(2,1)} %collective-permute-done.9, bf16[2,32,4,16,128]{1,2,4,3,0:T(4,128)(2,1)} %copy.493, bf16[2,32,4,1,128]{1,2,4,3,0:T(4,128)(2,1)S(1)} %collective-permute-done.8), kind=kLoop, calls=%fused_computation.1 | loop fusion | flops 1179648 | bytes 2359296 | tf_op jit(solution)/shard_map/concatenate | solution.py:19
  178.3 3.6 collective-permute-start.10
  185.6 2.2 dot_general.394
  195.3 7.1 %copy.497 = bf16[2,32,4,18,128]{4,1,3,2,0:T(8,128)(2,1)} copy(bf16[2,32,4,18,128]{1,2,4,3,0:T(4,128)(2,1)} %copy-done.1) | data formatting | bytes 2359296 | tf_op jit(solution)/shard_map/concatenate | solution.py:19
  204.4 2.6 pad_maximum_fusion.3
  209.0 3.1 fusion.173
  213.3 3.0 fusion.171
  243.7 2.2 dot_general.408
  249.7 2.2 dot_general.404
  257.3 44.2 %all-reduce.2 = (f32[2,32]{1,0:T(2,128)S(1)}, f32[2,32]{1,0:T(2,128)S(1)}) all-reduce(f32[2,32]{1,0:T(2,128)S(1)} %pad_maximum_fusion.77, f32[2,32]{1,0:T(2,128)S(1)} %pad_maximum_fusion.76), channel_id=1, replica_groups=mesh['gx'=4,'gy'=4,'gz'=2] {'gx','gy','gz'}, use_global_device_ids=true, to_apply=%region_11.0 | all-reduce | flops 128 | bytes 1024 | tf_op jit(solution)/shard_map/psum | solution.py:88
  303.6 38.6 %all-reduce.1 = (f32[32]{0:T(128)S(1)}, f32[32]{0:T(128)S(1)}) all-reduce(f32[32]{0:T(128)S(1)} %get-tuple-element.28, f32[32]{0:T(128)S(1)} %get-tuple-element.27), channel_id=1, replica_groups=mesh['gx'=4,'gy'=4,'gz'=2] {'gx','gy','gz'}, use_global_device_ids=true, to_apply=%region_15.0 | all-reduce | flops 64 | bytes 512 | tf_op jit(solution)/shard_map/psum | solution.py:101
  345.7 3.7 collective-permute-start.12
  361.8 2.7 collective-permute-done.15
  368.1 5.1 collective-permute-start.16
  376.8 2.2 maximum_maximum_fusion
  387.8 43.2 %all-reduce = (f32[32]{0:T(128)S(1)}, f32[32]{0:T(128)S(1)}) all-reduce(f32[32]{0:T(128)S(1)} %get-tuple-element.26, f32[32]{0:T(128)S(1)} %get-tuple-element.25), channel_id=1, replica_groups=mesh['gx'=4,'gy'=4,'gz'=2] {'gx','gy','gz'}, use_global_device_ids=true, to_apply=%region_19.20 | all-reduce | flops 64 | bytes 512 | tf_op jit(solution)/shard_map/psum | solution.py:101
  445.5 3.7 collective-permute-done.21
  452.2 4.5 collective-permute-start.22
  469.4 105.3 %all-reduce.7.cloned.1.call-done = (f32[3,3,3,32,32]{4,3,2,1,0:T(8,128)}, f32[3,3,3,32,32]{4,3,2,1,0:T(8,128)}) async-done(((f32[3,3,3,32,32]{4,3,2,1,0:T(8,128)}, f32[3,3,3,32,32]{4,3,2,1,0:T(8,128)}), (f32[3,3,3,32,32]{4,3,2,1,0:T(8,128)}, f32[3,3,3,32,32]{4,3,2,1,0:T(8,128)})) %all-reduce.7.cloned.1.call-update) | async-done | bytes 221200 | tf_op jit(solution)/shard_map/psum | solution.py:149
  (655 shorter events, 186.4 us)
Async XLA Ops:
  7.2 567.6 %all-reduce.7.cloned.1.call-start = ((), (), s32[]{:S(2)}) async-start(), calls=%async_computation | async-start | bytes 1769472 | tf_op jit(solution)/shard_map/psum | solution.py:149
  8.4 10.5 %collective-permute-start = (bf16[2,32,1,16,128]{4,3,2,1,0:T(8,128)(2,1)S(1)}, bf16[2,32,1,16,128]{4,3,2,1,0:T(8,128)(2,1)S(1)}, u32[]{:S(2)}, u32[]{:S(2)}) collective-permute-start(bf16[2,32,1,16,128]{4,3,2,1,0:T(8,128)(2,1)S(1)} %get-tuple-element.227), channel_id=1, source_target_pairs={{0,8},{8,16},{16,24},{1,9},{9,17},{17,25},{2,10},{10,18},{18,26},{... | collective-permute-start | bytes 786440 | tf_op jit(solution)/shard_map/ppermute | solution.py:15
  13.4 9.7 %collective-permute-start.1 = (bf16[2,32,1,16,128]{4,3,2,1,0:T(8,128)(2,1)S(1)}, bf16[2,32,1,16,128]{4,3,2,1,0:T(8,128)(2,1)S(1)}, u32[]{:S(2)}, u32[]{:S(2)}) collective-permute-start(bf16[2,32,1,16,128]{4,3,2,1,0:T(8,128)(2,1)S(1)} %get-tuple-element.228), channel_id=1, source_target_pairs={{8,0},{16,8},{24,16},{9,1},{17,9},{25,17},{10,2},{18,10},{26,18},{... | collective-permute-start | bytes 786440 | tf_op jit(solution)/shard_map/ppermute | solution.py:18
  28.2 3.3 collective-permute-start.2
  29.5 5.1 collective-permute-start.3
  43.0 18.5 %collective-permute-start.4 = (bf16[2,32,4,18,1]{1,2,4,3,0:T(4,128)(2,1)S(1)}, bf16[2,32,4,18,1]{1,2,4,3,0:T(4,128)(2,1)}, u32[]{:S(2)}, u32[]{:S(2)}) collective-permute-start(bf16[2,32,4,18,1]{1,2,4,3,0:T(4,128)(2,1)S(1)} %get-tuple-element.43), channel_id=1, source_target_pairs={{0,1},{2,3},{4,5},{6,7},{8,9},{10,11},{12,13},{14,15},{16,17},{18,... | collective-permute-start | bytes 27656 | tf_op jit(solution)/shard_map/ppermute | solution.py:15
  47.0 13.5 %collective-permute-start.5 = (bf16[2,32,4,18,1]{1,2,4,3,0:T(4,128)(2,1)S(1)}, bf16[2,32,4,18,1]{1,2,4,3,0:T(4,128)(2,1)S(1)}, u32[]{:S(2)}, u32[]{:S(2)}) collective-permute-start(bf16[2,32,4,18,1]{1,2,4,3,0:T(4,128)(2,1)S(1)} %get-tuple-element.44), channel_id=1, source_target_pairs={{1,0},{3,2},{5,4},{7,6},{9,8},{11,10},{13,12},{15,14},{17,16},{19,... | collective-permute-start | bytes 27656 | tf_op jit(solution)/shard_map/ppermute | solution.py:18
  82.2 58.9 %copy-start.21 = (f32[4,8,32,128]{3,2,1,0:T(8,128)}, f32[4,8,32,128]{3,2,1,0:T(8,128)S(1)}, u32[]{:S(2)}) copy-start(f32[4,8,32,128]{3,2,1,0:T(8,128)S(1)} %copy.596) | copy-start | bytes 1572868
  92.2 48.9 %copy-start.147 = (f32[32]{0:T(128)S(1)}, f32[32]{0:T(128)}, u32[]{:S(2)}) copy-start(f32[32]{0:T(128)} %param.14) | copy-start | bytes 388
  92.2 48.9 %copy-start.149 = (f32[32]{0:T(128)S(1)}, f32[32]{0:T(128)}, u32[]{:S(2)}) copy-start(f32[32]{0:T(128)} %param.13) | copy-start | bytes 388
  141.6 6.9 %collective-permute-start.6 = (bf16[2,32,1,16,128]{4,3,2,1,0:T(8,128)(2,1)S(1)}, bf16[2,32,1,16,128]{4,3,2,1,0:T(8,128)(2,1)S(1)}, u32[]{:S(2)}, u32[]{:S(2)}) collective-permute-start(bf16[2,32,1,16,128]{4,3,2,1,0:T(8,128)(2,1)S(1)} %get-tuple-element.225), channel_id=1, source_target_pairs={{0,8},{8,16},{16,24},{1,9},{9,17},{17,25},{2,10},{10,18},{18,26},{... | collective-permute-start | bytes 786440 | tf_op jit(solution)/shard_map/ppermute | solution.py:15
  143.8 8.8 %collective-permute-start.7 = (bf16[2,32,1,16,128]{4,3,2,1,0:T(8,128)(2,1)S(1)}, bf16[2,32,1,16,128]{4,3,2,1,0:T(8,128)(2,1)S(1)}, u32[]{:S(2)}, u32[]{:S(2)}) collective-permute-start(bf16[2,32,1,16,128]{4,3,2,1,0:T(8,128)(2,1)S(1)} %get-tuple-element.226), channel_id=1, source_target_pairs={{8,0},{16,8},{24,16},{9,1},{17,9},{25,17},{10,2},{18,10},{26,18},{... | collective-permute-start | bytes 786440 | tf_op jit(solution)/shard_map/ppermute | solution.py:18
  161.5 8.3 %collective-permute-start.8 = (bf16[2,32,4,1,128]{1,2,4,3,0:T(4,128)(2,1)}, bf16[2,32,4,1,128]{1,2,4,3,0:T(4,128)(2,1)S(1)}, u32[]{:S(2)}, u32[]{:S(2)}) collective-permute-start(bf16[2,32,4,1,128]{1,2,4,3,0:T(4,128)(2,1)} %get-tuple-element.45), channel_id=1, source_target_pairs={{0,2},{2,4},{4,6},{1,3},{3,5},{5,7},{8,10},{10,12},{12,14},{9,11},... | collective-permute-start | bytes 196616 | tf_op jit(solution)/shard_map/ppermute | solution.py:15
  162.8 7.0 %collective-permute-start.9 = (bf16[2,32,4,1,128]{1,2,4,3,0:T(4,128)(2,1)}, bf16[2,32,4,1,128]{1,2,4,3,0:T(4,128)(2,1)}, u32[]{:S(2)}, u32[]{:S(2)}) collective-permute-start(bf16[2,32,4,1,128]{1,2,4,3,0:T(4,128)(2,1)} %get-tuple-element.46), channel_id=1, source_target_pairs={{2,0},{4,2},{6,4},{3,1},{5,3},{7,5},{10,8},{12,10},{14,12},{11,9},... | collective-permute-start | bytes 196616 | tf_op jit(solution)/shard_map/ppermute | solution.py:18
  178.3 25.1 %collective-permute-start.10 = (bf16[2,32,4,18,1]{1,2,4,3,0:T(4,128)(2,1)S(1)}, bf16[2,32,4,18,1]{1,2,4,3,0:T(4,128)(2,1)S(1)}, u32[]{:S(2)}, u32[]{:S(2)}) collective-permute-start(bf16[2,32,4,18,1]{1,2,4,3,0:T(4,128)(2,1)S(1)} %get-tuple-element.41), channel_id=1, source_target_pairs={{0,1},{2,3},{4,5},{6,7},{8,9},{10,11},{12,13},{14,15},{16,17},{18,... | collective-permute-start | bytes 27656 | tf_op jit(solution)/shard_map/ppermute | solution.py:15
  181.9 20.5 %collective-permute-start.11 = (bf16[2,32,4,18,1]{1,2,4,3,0:T(4,128)(2,1)S(1)}, bf16[2,32,4,18,1]{1,2,4,3,0:T(4,128)(2,1)S(1)}, u32[]{:S(2)}, u32[]{:S(2)}) collective-permute-start(bf16[2,32,4,18,1]{1,2,4,3,0:T(4,128)(2,1)S(1)} %get-tuple-element.42), channel_id=1, source_target_pairs={{1,0},{3,2},{5,4},{7,6},{9,8},{11,10},{13,12},{15,14},{17,16},{19,... | collective-permute-start | bytes 27656 | tf_op jit(solution)/shard_map/ppermute | solution.py:18
  256.6 44.9 %copy-start.152 = (f32[32]{0:T(128)S(1)}, f32[32]{0:T(128)}, u32[]{:S(2)}) copy-start(f32[32]{0:T(128)} %param.15) | copy-start | bytes 388
  256.6 45.1 %copy-start.106 = (bf16[32,2,16,128]{3,2,1,0:T(8,128)(2,1)S(1)}, bf16[32,2,16,128]{3,2,1,0:T(8,128)(2,1)}, u32[]{:S(2)}) copy-start(bf16[32,2,16,128]{3,2,1,0:T(8,128)(2,1)} %param.17) | copy-start | bytes 786436
  256.6 45.1 %copy-start.151 = (f32[32]{0:T(128)S(1)}, f32[32]{0:T(128)}, u32[]{:S(2)}) copy-start(f32[32]{0:T(128)} %param.16) | copy-start | bytes 388
  257.2 44.5 %copy-start.43 = (f32[4,8,32,128]{3,2,1,0:T(8,128)S(1)}, f32[4,8,32,128]{3,2,1,0:T(8,128)}, u32[]{:S(2)}) copy-start(f32[4,8,32,128]{3,2,1,0:T(8,128)} %copy.606) | copy-start | bytes 1572868
  345.7 11.9 %collective-permute-start.12 = (bf16[32,1,16,128]{3,0,2,1:T(8,128)(2,1)}, bf16[32,1,16,128]{3,0,2,1:T(8,128)(2,1)S(1)}, u32[]{:S(2)}, u32[]{:S(2)}) collective-permute-start(bf16[32,1,16,128]{3,0,2,1:T(8,128)(2,1)} %get-tuple-element.237), channel_id=1, source_target_pairs={{0,8},{8,16},{16,24},{1,9},{9,17},{17,25},{2,10},{10,18},{18,26},{... | collective-permute-start | bytes 393224 | tf_op jit(solution)/shard_map/ppermute | solution.py:15
  349.4 8.2 %collective-permute-start.13 = (bf16[32,1,16,128]{3,0,2,1:T(8,128)(2,1)S(1)}, bf16[32,1,16,128]{3,0,2,1:T(8,128)(2,1)S(1)}, u32[]{:S(2)}, u32[]{:S(2)}) collective-permute-start(bf16[32,1,16,128]{3,0,2,1:T(8,128)(2,1)S(1)} %get-tuple-element.238), channel_id=1, source_target_pairs={{8,0},{16,8},{24,16},{9,1},{17,9},{25,17},{10,2},{18,10},{26,18},{... | collective-permute-start | bytes 393224 | tf_op jit(solution)/shard_map/ppermute | solution.py:18
  357.6 4.2 collective-permute-start.14
  358.9 5.6 collective-permute-start.15
  366.8 8.7 %collective-permute-start.17 = (bf16[32,4,18,1]{0,2,3,1:T(8,128)(2,1)S(1)}, bf16[32,4,18,1]{0,2,3,1:T(8,128)(2,1)}, u32[]{:S(2)}, u32[]{:S(2)}) collective-permute-start(bf16[32,4,18,1]{0,2,3,1:T(8,128)(2,1)S(1)} %copy.531), channel_id=1, source_target_pairs={{1,0},{3,2},{5,4},{7,6},{9,8},{11,10},{13,12},{15,14},{17,16},{19,... | collective-permute-start | bytes 13832 | tf_op jit(solution)/shard_map/ppermute | solution.py:18
  368.1 6.8 %collective-permute-start.16 = (bf16[32,4,18,1]{0,2,3,1:T(8,128)(2,1)}, bf16[32,4,18,1]{0,2,3,1:T(8,128)(2,1)S(1)}, u32[]{:S(2)}, u32[]{:S(2)}) collective-permute-start(bf16[32,4,18,1]{0,2,3,1:T(8,128)(2,1)} %copy.529), channel_id=1, source_target_pairs={{0,1},{2,3},{4,5},{6,7},{8,9},{10,11},{12,13},{14,15},{16,17},{18,... | collective-permute-start | bytes 13832 | tf_op jit(solution)/shard_map/ppermute | solution.py:15
  432.1 10.2 %collective-permute-start.18 = (bf16[32,1,16,128]{3,0,2,1:T(8,128)(2,1)S(1)}, bf16[32,1,16,128]{3,0,2,1:T(8,128)(2,1)S(1)}, u32[]{:S(2)}, u32[]{:S(2)}) collective-permute-start(bf16[32,1,16,128]{3,0,2,1:T(8,128)(2,1)S(1)} %get-tuple-element.232), channel_id=1, source_target_pairs={{0,8},{8,16},{16,24},{1,9},{9,17},{17,25},{2,10},{10,18},{18,26},{... | collective-permute-start | bytes 393224 | tf_op jit(solution)/shard_map/ppermute | solution.py:15
  434.2 8.1 %collective-permute-start.19 = (bf16[32,1,16,128]{3,0,2,1:T(8,128)(2,1)S(1)}, bf16[32,1,16,128]{3,0,2,1:T(8,128)(2,1)S(1)}, u32[]{:S(2)}, u32[]{:S(2)}) collective-permute-start(bf16[32,1,16,128]{3,0,2,1:T(8,128)(2,1)S(1)} %get-tuple-element.233), channel_id=1, source_target_pairs={{8,0},{16,8},{24,16},{9,1},{17,9},{25,17},{10,2},{18,10},{26,18},{... | collective-permute-start | bytes 393224 | tf_op jit(solution)/shard_map/ppermute | solution.py:18
  442.3 3.2 collective-permute-start.20
  443.6 5.6 collective-permute-start.21
  450.9 7.9 %collective-permute-start.23 = (bf16[32,4,18,1]{0,2,3,1:T(8,128)(2,1)S(1)}, bf16[32,4,18,1]{0,2,3,1:T(8,128)(2,1)S(1)}, u32[]{:S(2)}, u32[]{:S(2)}) collective-permute-start(bf16[32,4,18,1]{0,2,3,1:T(8,128)(2,1)S(1)} %copy.546), channel_id=1, source_target_pairs={{1,0},{3,2},{5,4},{7,6},{9,8},{11,10},{13,12},{15,14},{17,16},{19,... | collective-permute-start | bytes 13832 | tf_op jit(solution)/shard_map/ppermute | solution.py:18
  452.2 6.1 %collective-permute-start.22 = (bf16[32,4,18,1]{0,2,3,1:T(8,128)(2,1)S(1)}, bf16[32,4,18,1]{0,2,3,1:T(8,128)(2,1)S(1)}, u32[]{:S(2)}, u32[]{:S(2)}) collective-permute-start(bf16[32,4,18,1]{0,2,3,1:T(8,128)(2,1)S(1)} %copy.544), channel_id=1, source_target_pairs={{0,1},{2,3},{4,5},{6,7},{8,9},{10,11},{12,13},{14,15},{16,17},{18,... | collective-permute-start | bytes 13832 | tf_op jit(solution)/shard_map/ppermute | solution.py:15
  (146 other events, 433.2 us)
Sparse Core Ops, SparseCore 0:
  442.4 132.2 all-reduce.6
where the time goes:
time: 592 us; the launch traced here: 585 us
  blocking collectives  170 us (29%)
  local copies, waits for them, and re-layouts  139 us (23%)
  waiting for transfers between devices  131 us (22%)
  starting transfers between devices  51.5 us (9%)
  other arithmetic  40.1 us (7%)
  matrix products  36.3 us (6%)
  between operations  17.5 us (3%)
    psum x1, waiting for transfers between devices, body(): grad_w_first = lax.psum(local_first, ('gx', 'gy', 'gz'))  105 us
    psum x2, blocking collectives, statistics(): sums, squares = lax.psum((local_sums, local_squares), ('gx', 'gy', 'gz'))  88.7 us
    psum x2, blocking collectives, backward_layer(): lax.psum((jnp.sum(slope, axis=(1, 2, 3)), jnp.sum(slope * normed, axis=(1...  81.7 us
    ppermute x12, starting transfers between devices, extended(): lax.ppermute(lax.slice_in_dim(block, block.shape[dim] - width, None, axis...  35.5 us
    dot_general x18, local copies, waits for them, and re-layouts, kernel_grad(): lax.dot_general(flat, stacked, (((1,), (1,)), ((), ())), preferred_elemen...  25 us
    dot_general x54, matrix products, convolve(): total = total + jnp.dot(matrix, stacked, preferred_element_type=jnp.float32)  24.8 us
    unnamed x315, local copies, waits for them, and re-layouts  23.4 us
    concatenate x4, local copies, waits for them, and re-layouts, extended(): block = jnp.concatenate([low, block, high], axis=dim)  22.8 us
  transfers between devices with their start and end apart: 25, of which 10 were waited for; matrix products, arithmetic and copies ran while one was open for 12% of the time, Pallas kernels for 0%

commit v1 on v0

--- a/solution.py
+++ b/solution.py
@@ -5,6 +5,7 @@
 from jax.sharding import PartitionSpec as P
 
 EPSILON = 1e-05
+replace_the_axis_part = lambda local_values: lax.psum(lax.psum(local_values, "gx"), ("gy", "gz"))
 
 
 def extended(block, sides, width):
@@ -98,9 +99,8 @@
 
 def backward_layer(upstream, preact, normed, scales, gain, voxels):
     slope = upstream * silu_slope(preact)
-    sum_d, sum_dx = lax.psum(
-        (jnp.sum(slope, axis=(1, 2, 3)), jnp.sum(slope * normed, axis=(1, 2, 3))),
-        ("gx", "gy", "gz"),
+    sum_d, sum_dx = replace_the_axis_part(
+        (jnp.sum(slope, axis=(1, 2, 3)), jnp.sum(slope * normed, axis=(1, 2, 3)))
     )
     delta = spread(gain * scales) * (
         slope - spread(sum_d / voxels) - normed * spread(sum_dx / voxels)

time: 592 us -> 554 us (0.936)
  blocking collectives: 170 us -> 139 us
    psum x2 -> x4, blocking collectives: 81.7 us -> 50.7 us  [the longest x2 29 us: lax.psum(lax.psum(local_values, 'gx'), ('gy', 'gz'))]
  transfers between devices with their start and end apart: 25 -> 25, of which waited for: 10 -> 10; matrix products, arithmetic and copies ran while one was open for 12% -> 13% of each run, Pallas kernels for 0% -> 0%
where the time goes in v1:
time: 554 us; the launch traced here: 547 us
  local copies, waits for them, and re-layouts  139 us (25%)
  blocking collectives  139 us (25%)
  waiting for transfers between devices  126 us (23%)
  starting transfers between devices  49.9 us (9%)
  other arithmetic  40.1 us (7%)
  matrix products  36.3 us (7%)
  between operations  17.5 us (3%)
    psum x1, waiting for transfers between devices, body(): grad_w_first = lax.psum(local_first, ('gx', 'gy', 'gz'))  103 us
    psum x2, blocking collectives, statistics(): sums, squares = lax.psum((local_sums, local_squares), ('gx', 'gy', 'gz'))  88.7 us
    ppermute x12, starting transfers between devices, extended(): lax.ppermute(lax.slice_in_dim(block, block.shape[dim] - width, None, axis...  33.8 us
    psum x2, blocking collectives, lax.psum(lax.psum(local_values, 'gx'), ('gy', 'gz'))  29 us
    dot_general x18, local copies, waits for them, and re-layouts, kernel_grad(): lax.dot_general(flat, stacked, (((1,), (1,)), ((), ())), preferred_elemen...  25 us
    dot_general x54, matrix products, convolve(): total = total + jnp.dot(matrix, stacked, preferred_element_type=jnp.float32)  24.8 us
    unnamed x315, local copies, waits for them, and re-layouts  23.4 us
    concatenate x4, local copies, waits for them, and re-layouts, extended(): block = jnp.concatenate([low, block, high], axis=dim)  22.8 us
  transfers between devices with their start and end apart: 25, of which 10 were waited for; matrix products, arithmetic and copies ran while one was open for 13% of the time, Pallas kernels for 0%

profile of v1, /device:TPU:0, one launch (start us, length us, event | category | flops | bytes accessed | tf_op | source)
XLA Modules:
  0.0 547.5 jit_solution(11806351981170898260)
XLA Ops:
  8.4 5.0 collective-permute-start
  15.6 3.3 collective-permute-done
  18.9 4.1 collective-permute-done.1
  23.2 3.7 copy.460
  31.5 3.1 collective-permute-done.3
  34.6 6.2 %pad_maximum_fusion = bf16[2,32,4,18,128]{1,2,4,3,0:T(4,128)(2,1)S(1)} fusion(bf16[2,32,4,1,128]{1,2,4,3,0:T(4,128)(2,1)S(1)} %collective-permute-done.3, bf16[2,32,4,16,128]{1,2,4,3,0:T(4,128)(2,1)} %copy.460, bf16[2,32,4,1,128]{1,2,4,3,0:T(4,128)(2,1)S(1)} %collective-permute-done.2), kind=kLoop, calls=%fused_computation | loop fusion | flops 1179648 | bytes 2359296 | tf_op jit(solution)/shard_map/concatenate | solution.py:20
  43.0 4.0 collective-permute-start.4
  54.2 6.3 %copy.464 = bf16[2,32,4,18,128]{4,1,3,2,0:T(8,128)(2,1)S(1)} copy(bf16[2,32,4,18,128]{1,2,4,3,0:T(4,128)(2,1)} %copy-done) | data formatting | bytes 2359296 | tf_op jit(solution)/shard_map/concatenate | solution.py:20
  67.7 3.2 fusion.175
  94.8 44.5 %all-reduce.1 = (f32[2,32]{1,0:T(2,128)S(1)}, f32[2,32]{1,0:T(2,128)S(1)}) all-reduce(f32[2,32]{1,0:T(2,128)S(1)} %pad_maximum_fusion.75, f32[2,32]{1,0:T(2,128)S(1)} %pad_maximum_fusion.74), channel_id=1, replica_groups=mesh['gx'=4,'gy'=4,'gz'=2] {'gx','gy','gz'}, use_global_device_ids=true, to_apply=%region_5.0 | all-reduce | flops 128 | bytes 1024 | tf_op jit(solution)/shard_map/psum | solution.py:89
  145.9 2.7 collective-permute-done.6
  148.5 4.1 collective-permute-done.7
  153.8 5.6 %copy.493 = bf16[2,32,4,16,128]{1,2,4,3,0:T(4,128)(2,1)} copy(bf16[2,32,4,16,128]{4,3,2,1,0:T(8,128)(2,1)} %pad_maximum_fusion.7) | data formatting | bytes 2097152 | tf_op jit(solution)/shard_map/concatenate | solution.py:20
  169.8 6.3 %pad_maximum_fusion.1 = bf16[2,32,4,18,128]{1,2,4,3,0:T(4,128)(2,1)S(1)} fusion(bf16[2,32,4,1,128]{1,2,4,3,0:T(4,128)(2,1)} %collective-permute-done.9, bf16[2,32,4,16,128]{1,2,4,3,0:T(4,128)(2,1)} %copy.493, bf16[2,32,4,1,128]{1,2,4,3,0:T(4,128)(2,1)S(1)} %collective-permute-done.8), kind=kLoop, calls=%fused_computation.1 | loop fusion | flops 1179648 | bytes 2359296 | tf_op jit(solution)/shard_map/concatenate | solution.py:20
  178.3 3.6 collective-permute-start.10
  185.6 2.2 dot_general.394
  195.2 7.1 %copy.497 = bf16[2,32,4,18,128]{4,1,3,2,0:T(8,128)(2,1)} copy(bf16[2,32,4,18,128]{1,2,4,3,0:T(4,128)(2,1)} %copy-done.1) | data formatting | bytes 2359296 | tf_op jit(solution)/shard_map/concatenate | solution.py:20
  204.3 2.6 pad_maximum_fusion.3
  208.9 3.1 fusion.173
  213.2 3.0 fusion.171
  243.6 2.2 dot_general.408
  249.6 2.2 dot_general.404
  257.3 44.2 %all-reduce = (f32[2,32]{1,0:T(2,128)S(1)}, f32[2,32]{1,0:T(2,128)S(1)}) all-reduce(f32[2,32]{1,0:T(2,128)S(1)} %pad_maximum_fusion.77, f32[2,32]{1,0:T(2,128)S(1)} %pad_maximum_fusion.76), channel_id=1, replica_groups=mesh['gx'=4,'gy'=4,'gz'=2] {'gx','gy','gz'}, use_global_device_ids=true, to_apply=%region_11.0 | all-reduce | flops 128 | bytes 1024 | tf_op jit(solution)/shard_map/psum | solution.py:89
  303.5 10.6 %all-reduce.6 = (f32[32]{0:T(128)S(1)}, f32[32]{0:T(128)S(1)}) all-reduce(f32[32]{0:T(128)S(1)} %get-tuple-element.28, f32[32]{0:T(128)S(1)} %get-tuple-element.27), channel_id=1, replica_groups=mesh['gx'=4,'gy'=4,'gz'=2] {'gx'}, use_global_device_ids=true, to_apply=%region_16.0 | all-reduce | flops 64 | bytes 512 | tf_op jit(solution)/shard_map/psum | solution.py:8
  314.1 14.3 %all-reduce.4 = (f32[32]{0:T(128)S(1)}, f32[32]{0:T(128)S(1)}) all-reduce(f32[32]{0:T(128)S(1)} %get-tuple-element.41, f32[32]{0:T(128)S(1)} %get-tuple-element.42), channel_id=1, replica_groups=mesh['gx'=4,'gy'=4,'gz'=2] {'gy','gz'}, use_global_device_ids=true, to_apply=%region_17.0 | all-reduce | flops 64 | bytes 512 | tf_op jit(solution)/shard_map/psum | solution.py:8
  350.2 5.1 collective-permute-start.16
  358.9 2.2 maximum_maximum_fusion
  370.0 11.1 %all-reduce.5 = (f32[32]{0:T(128)S(1)}, f32[32]{0:T(128)S(1)}) all-reduce(f32[32]{0:T(128)S(1)} %get-tuple-element.26, f32[32]{0:T(128)S(1)} %get-tuple-element.25), channel_id=1, replica_groups=mesh['gx'=4,'gy'=4,'gz'=2] {'gx'}, use_global_device_ids=true, to_apply=%region_22.23 | all-reduce | flops 64 | bytes 512 | tf_op jit(solution)/shard_map/psum | solution.py:8
  381.1 14.7 %all-reduce.3 = (f32[32]{0:T(128)S(1)}, f32[32]{0:T(128)S(1)}) all-reduce(f32[32]{0:T(128)S(1)} %get-tuple-element.39, f32[32]{0:T(128)S(1)} %get-tuple-element.40), channel_id=1, replica_groups=mesh['gx'=4,'gy'=4,'gz'=2] {'gy','gz'}, use_global_device_ids=true, to_apply=%region_23.24 | all-reduce | flops 64 | bytes 512 | tf_op jit(solution)/shard_map/psum | solution.py:8
  410.2 3.0 collective-permute-done.21
  416.1 4.5 collective-permute-start.22
  433.4 103.4 %all-reduce.9.cloned.1.call-done = (f32[3,3,3,32,32]{4,3,2,1,0:T(8,128)}, f32[3,3,3,32,32]{4,3,2,1,0:T(8,128)}) async-done(((f32[3,3,3,32,32]{4,3,2,1,0:T(8,128)}, f32[3,3,3,32,32]{4,3,2,1,0:T(8,128)}), (f32[3,3,3,32,32]{4,3,2,1,0:T(8,128)}, f32[3,3,3,32,32]{4,3,2,1,0:T(8,128)})) %all-reduce.9.cloned.1.call-update) | async-done | bytes 221200 | tf_op jit(solution)/shard_map/psum | solution.py:149
  (657 shorter events, 188.6 us)
Async XLA Ops:
  7.2 529.6 %all-reduce.9.cloned.1.call-start = ((), (), s32[]{:S(2)}) async-start(), calls=%async_computation | async-start | bytes 1769472 | tf_op jit(solution)/shard_map/psum | solution.py:149
  8.4 10.5 %collective-permute-start = (bf16[2,32,1,16,128]{4,3,2,1,0:T(8,128)(2,1)S(1)}, bf16[2,32,1,16,128]{4,3,2,1,0:T(8,128)(2,1)S(1)}, u32[]{:S(2)}, u32[]{:S(2)}) collective-permute-start(bf16[2,32,1,16,128]{4,3,2,1,0:T(8,128)(2,1)S(1)} %get-tuple-element.231), channel_id=1, source_target_pairs={{0,8},{8,16},{16,24},{1,9},{9,17},{17,25},{2,10},{10,18},{18,26},{... | collective-permute-start | bytes 786440 | tf_op jit(solution)/shard_map/ppermute | solution.py:16
  13.4 9.7 %collective-permute-start.1 = (bf16[2,32,1,16,128]{4,3,2,1,0:T(8,128)(2,1)S(1)}, bf16[2,32,1,16,128]{4,3,2,1,0:T(8,128)(2,1)S(1)}, u32[]{:S(2)}, u32[]{:S(2)}) collective-permute-start(bf16[2,32,1,16,128]{4,3,2,1,0:T(8,128)(2,1)S(1)} %get-tuple-element.232), channel_id=1, source_target_pairs={{8,0},{16,8},{24,16},{9,1},{17,9},{25,17},{10,2},{18,10},{26,18},{... | collective-permute-start | bytes 786440 | tf_op jit(solution)/shard_map/ppermute | solution.py:19
  28.2 3.3 collective-permute-start.2
  29.5 5.1 collective-permute-start.3
  43.0 18.5 %collective-permute-start.4 = (bf16[2,32,4,18,1]{1,2,4,3,0:T(4,128)(2,1)S(1)}, bf16[2,32,4,18,1]{1,2,4,3,0:T(4,128)(2,1)}, u32[]{:S(2)}, u32[]{:S(2)}) collective-permute-start(bf16[2,32,4,18,1]{1,2,4,3,0:T(4,128)(2,1)S(1)} %get-tuple-element.47), channel_id=1, source_target_pairs={{0,1},{2,3},{4,5},{6,7},{8,9},{10,11},{12,13},{14,15},{16,17},{18,... | collective-permute-start | bytes 27656 | tf_op jit(solution)/shard_map/ppermute | solution.py:16
  47.0 13.5 %collective-permute-start.5 = (bf16[2,32,4,18,1]{1,2,4,3,0:T(4,128)(2,1)S(1)}, bf16[2,32,4,18,1]{1,2,4,3,0:T(4,128)(2,1)S(1)}, u32[]{:S(2)}, u32[]{:S(2)}) collective-permute-start(bf16[2,32,4,18,1]{1,2,4,3,0:T(4,128)(2,1)S(1)} %get-tuple-element.48), channel_id=1, source_target_pairs={{1,0},{3,2},{5,4},{7,6},{9,8},{11,10},{13,12},{15,14},{17,16},{19,... | collective-permute-start | bytes 27656 | tf_op jit(solution)/shard_map/ppermute | solution.py:19
  82.2 58.9 %copy-start.21 = (f32[4,8,32,128]{3,2,1,0:T(8,128)}, f32[4,8,32,128]{3,2,1,0:T(8,128)S(1)}, u32[]{:S(2)}) copy-start(f32[4,8,32,128]{3,2,1,0:T(8,128)S(1)} %copy.596) | copy-start | bytes 1572868
  92.2 48.9 %copy-start.147 = (f32[32]{0:T(128)S(1)}, f32[32]{0:T(128)}, u32[]{:S(2)}) copy-start(f32[32]{0:T(128)} %param.14) | copy-start | bytes 388
  92.2 48.9 %copy-start.149 = (f32[32]{0:T(128)S(1)}, f32[32]{0:T(128)}, u32[]{:S(2)}) copy-start(f32[32]{0:T(128)} %param.13) | copy-start | bytes 388
  141.6 6.9 %collective-permute-start.6 = (bf16[2,32,1,16,128]{4,3,2,1,0:T(8,128)(2,1)S(1)}, bf16[2,32,1,16,128]{4,3,2,1,0:T(8,128)(2,1)S(1)}, u32[]{:S(2)}, u32[]{:S(2)}) collective-permute-start(bf16[2,32,1,16,128]{4,3,2,1,0:T(8,128)(2,1)S(1)} %get-tuple-element.229), channel_id=1, source_target_pairs={{0,8},{8,16},{16,24},{1,9},{9,17},{17,25},{2,10},{10,18},{18,26},{... | collective-permute-start | bytes 786440 | tf_op jit(solution)/shard_map/ppermute | solution.py:16
  143.8 8.8 %collective-permute-start.7 = (bf16[2,32,1,16,128]{4,3,2,1,0:T(8,128)(2,1)S(1)}, bf16[2,32,1,16,128]{4,3,2,1,0:T(8,128)(2,1)S(1)}, u32[]{:S(2)}, u32[]{:S(2)}) collective-permute-start(bf16[2,32,1,16,128]{4,3,2,1,0:T(8,128)(2,1)S(1)} %get-tuple-element.230), channel_id=1, source_target_pairs={{8,0},{16,8},{24,16},{9,1},{17,9},{25,17},{10,2},{18,10},{26,18},{... | collective-permute-start | bytes 786440 | tf_op jit(solution)/shard_map/ppermute | solution.py:19
  161.5 8.3 %collective-permute-start.8 = (bf16[2,32,4,1,128]{1,2,4,3,0:T(4,128)(2,1)}, bf16[2,32,4,1,128]{1,2,4,3,0:T(4,128)(2,1)S(1)}, u32[]{:S(2)}, u32[]{:S(2)}) collective-permute-start(bf16[2,32,4,1,128]{1,2,4,3,0:T(4,128)(2,1)} %get-tuple-element.49), channel_id=1, source_target_pairs={{0,2},{2,4},{4,6},{1,3},{3,5},{5,7},{8,10},{10,12},{12,14},{9,11},... | collective-permute-start | bytes 196616 | tf_op jit(solution)/shard_map/ppermute | solution.py:16
  162.8 7.0 %collective-permute-start.9 = (bf16[2,32,4,1,128]{1,2,4,3,0:T(4,128)(2,1)}, bf16[2,32,4,1,128]{1,2,4,3,0:T(4,128)(2,1)}, u32[]{:S(2)}, u32[]{:S(2)}) collective-permute-start(bf16[2,32,4,1,128]{1,2,4,3,0:T(4,128)(2,1)} %get-tuple-element.50), channel_id=1, source_target_pairs={{2,0},{4,2},{6,4},{3,1},{5,3},{7,5},{10,8},{12,10},{14,12},{11,9},... | collective-permute-start | bytes 196616 | tf_op jit(solution)/shard_map/ppermute | solution.py:19
  178.3 25.1 %collective-permute-start.10 = (bf16[2,32,4,18,1]{1,2,4,3,0:T(4,128)(2,1)S(1)}, bf16[2,32,4,18,1]{1,2,4,3,0:T(4,128)(2,1)S(1)}, u32[]{:S(2)}, u32[]{:S(2)}) collective-permute-start(bf16[2,32,4,18,1]{1,2,4,3,0:T(4,128)(2,1)S(1)} %get-tuple-element.45), channel_id=1, source_target_pairs={{0,1},{2,3},{4,5},{6,7},{8,9},{10,11},{12,13},{14,15},{16,17},{18,... | collective-permute-start | bytes 27656 | tf_op jit(solution)/shard_map/ppermute | solution.py:16
  181.9 20.5 %collective-permute-start.11 = (bf16[2,32,4,18,1]{1,2,4,3,0:T(4,128)(2,1)S(1)}, bf16[2,32,4,18,1]{1,2,4,3,0:T(4,128)(2,1)S(1)}, u32[]{:S(2)}, u32[]{:S(2)}) collective-permute-start(bf16[2,32,4,18,1]{1,2,4,3,0:T(4,128)(2,1)S(1)} %get-tuple-element.46), channel_id=1, source_target_pairs={{1,0},{3,2},{5,4},{7,6},{9,8},{11,10},{13,12},{15,14},{17,16},{19,... | collective-permute-start | bytes 27656 | tf_op jit(solution)/shard_map/ppermute | solution.py:19
  256.5 44.9 %copy-start.152 = (f32[32]{0:T(128)S(1)}, f32[32]{0:T(128)}, u32[]{:S(2)}) copy-start(f32[32]{0:T(128)} %param.15) | copy-start | bytes 388
  256.5 45.1 %copy-start.106 = (bf16[32,2,16,128]{3,2,1,0:T(8,128)(2,1)S(1)}, bf16[32,2,16,128]{3,2,1,0:T(8,128)(2,1)}, u32[]{:S(2)}) copy-start(bf16[32,2,16,128]{3,2,1,0:T(8,128)(2,1)} %param.17) | copy-start | bytes 786436
  256.6 45.1 %copy-start.151 = (f32[32]{0:T(128)S(1)}, f32[32]{0:T(128)}, u32[]{:S(2)}) copy-start(f32[32]{0:T(128)} %param.16) | copy-start | bytes 388
  257.1 44.5 %copy-start.43 = (f32[4,8,32,128]{3,2,1,0:T(8,128)S(1)}, f32[4,8,32,128]{3,2,1,0:T(8,128)}, u32[]{:S(2)}) copy-start(f32[4,8,32,128]{3,2,1,0:T(8,128)} %copy.606) | copy-start | bytes 1572868
  331.9 9.9 %collective-permute-start.12 = (bf16[32,1,16,128]{3,0,2,1:T(8,128)(2,1)}, bf16[32,1,16,128]{3,0,2,1:T(8,128)(2,1)S(1)}, u32[]{:S(2)}, u32[]{:S(2)}) collective-permute-start(bf16[32,1,16,128]{3,0,2,1:T(8,128)(2,1)} %get-tuple-element.241), channel_id=1, source_target_pairs={{0,8},{8,16},{16,24},{1,9},{9,17},{17,25},{2,10},{10,18},{18,26},{... | collective-permute-start | bytes 393224 | tf_op jit(solution)/shard_map/ppermute | solution.py:16
  333.7 8.2 %collective-permute-start.13 = (bf16[32,1,16,128]{3,0,2,1:T(8,128)(2,1)S(1)}, bf16[32,1,16,128]{3,0,2,1:T(8,128)(2,1)S(1)}, u32[]{:S(2)}, u32[]{:S(2)}) collective-permute-start(bf16[32,1,16,128]{3,0,2,1:T(8,128)(2,1)S(1)} %get-tuple-element.242), channel_id=1, source_target_pairs={{8,0},{16,8},{24,16},{9,1},{17,9},{25,17},{10,2},{18,10},{26,18},{... | collective-permute-start | bytes 393224 | tf_op jit(solution)/shard_map/ppermute | solution.py:19
  341.9 4.6 collective-permute-start.14
  343.6 3.1 collective-permute-start.15
  348.9 8.7 %collective-permute-start.17 = (bf16[32,4,18,1]{0,2,3,1:T(8,128)(2,1)S(1)}, bf16[32,4,18,1]{0,2,3,1:T(8,128)(2,1)}, u32[]{:S(2)}, u32[]{:S(2)}) collective-permute-start(bf16[32,4,18,1]{0,2,3,1:T(8,128)(2,1)S(1)} %copy.531), channel_id=1, source_target_pairs={{1,0},{3,2},{5,4},{7,6},{9,8},{11,10},{13,12},{15,14},{17,16},{19,... | collective-permute-start | bytes 13832 | tf_op jit(solution)/shard_map/ppermute | solution.py:19
  350.2 6.8 %collective-permute-start.16 = (bf16[32,4,18,1]{0,2,3,1:T(8,128)(2,1)}, bf16[32,4,18,1]{0,2,3,1:T(8,128)(2,1)S(1)}, u32[]{:S(2)}, u32[]{:S(2)}) collective-permute-start(bf16[32,4,18,1]{0,2,3,1:T(8,128)(2,1)} %copy.529), channel_id=1, source_target_pairs={{0,1},{2,3},{4,5},{6,7},{8,9},{10,11},{12,13},{14,15},{16,17},{18,... | collective-permute-start | bytes 13832 | tf_op jit(solution)/shard_map/ppermute | solution.py:16
  396.9 9.6 %collective-permute-start.18 = (bf16[32,1,16,128]{3,0,2,1:T(8,128)(2,1)S(1)}, bf16[32,1,16,128]{3,0,2,1:T(8,128)(2,1)S(1)}, u32[]{:S(2)}, u32[]{:S(2)}) collective-permute-start(bf16[32,1,16,128]{3,0,2,1:T(8,128)(2,1)S(1)} %get-tuple-element.236), channel_id=1, source_target_pairs={{0,8},{8,16},{16,24},{1,9},{9,17},{17,25},{2,10},{10,18},{18,26},{... | collective-permute-start | bytes 393224 | tf_op jit(solution)/shard_map/ppermute | solution.py:16
  398.4 8.1 %collective-permute-start.19 = (bf16[32,1,16,128]{3,0,2,1:T(8,128)(2,1)S(1)}, bf16[32,1,16,128]{3,0,2,1:T(8,128)(2,1)S(1)}, u32[]{:S(2)}, u32[]{:S(2)}) collective-permute-start(bf16[32,1,16,128]{3,0,2,1:T(8,128)(2,1)S(1)} %get-tuple-element.237), channel_id=1, source_target_pairs={{8,0},{16,8},{24,16},{9,1},{17,9},{25,17},{10,2},{18,10},{26,18},{... | collective-permute-start | bytes 393224 | tf_op jit(solution)/shard_map/ppermute | solution.py:19
  406.5 3.7 collective-permute-start.20
  408.3 4.8 collective-permute-start.21
  414.8 7.9 %collective-permute-start.23 = (bf16[32,4,18,1]{0,2,3,1:T(8,128)(2,1)S(1)}, bf16[32,4,18,1]{0,2,3,1:T(8,128)(2,1)S(1)}, u32[]{:S(2)}, u32[]{:S(2)}) collective-permute-start(bf16[32,4,18,1]{0,2,3,1:T(8,128)(2,1)S(1)} %copy.546), channel_id=1, source_target_pairs={{1,0},{3,2},{5,4},{7,6},{9,8},{11,10},{13,12},{15,14},{17,16},{19,... | collective-permute-start | bytes 13832 | tf_op jit(solution)/shard_map/ppermute | solution.py:19
  416.1 6.1 %collective-permute-start.22 = (bf16[32,4,18,1]{0,2,3,1:T(8,128)(2,1)S(1)}, bf16[32,4,18,1]{0,2,3,1:T(8,128)(2,1)S(1)}, u32[]{:S(2)}, u32[]{:S(2)}) collective-permute-start(bf16[32,4,18,1]{0,2,3,1:T(8,128)(2,1)S(1)} %copy.544), channel_id=1, source_target_pairs={{0,1},{2,3},{4,5},{6,7},{8,9},{10,11},{12,13},{14,15},{16,17},{18,... | collective-permute-start | bytes 13832 | tf_op jit(solution)/shard_map/ppermute | solution.py:16
  (146 other events, 407.9 us)
Sparse Core Ops, SparseCore 0:
  406.6 130.1 all-reduce.8
